TPU v7x, 32 devices: a whole 2x2x4 slice. The times are simulated.
32 devices in a mesh: ctx: 8 (over z, y), dp: 4 (over x, core).
Axes of the slice: x: 2, y: 2, z: 4, core: 2. Of those that a mesh axis runs over, the one named last changes fastest.
Arguments:
- tokens: bfloat16 [8, 512, 4096], P('dp', 'ctx'), may hold values from -6 to 6
- queries: bfloat16 [8, 512, 2048], P('dp', 'ctx'), may hold values from -160 to 160
- d_attended: bfloat16 [8, 512, 2048], P('dp', 'ctx'), may hold values from -6 to 6
- span_order: int32 [16], replicated, may hold values from 0 to 15, each once
- norm_gain: float32 [4096], replicated, may hold values from 0.1 to 1.9
- key_weight: bfloat16 [4096, 512], replicated, may hold values from -0.09375 to 0.09375
- value_weight: bfloat16 [4096, 512], replicated, may hold values from -0.09375 to 0.09375
Outputs:
- attended: bfloat16 [8, 512, 2048], P('dp', 'ctx')
- grad_queries: bfloat16 [8, 512, 2048], P('dp', 'ctx')
- grad_tokens: bfloat16 [8, 512, 4096], P('dp', 'ctx')
- grad_key_weight: float32 [4096, 512], P(('ctx', 'dp'))
- grad_value_weight: float32 [4096, 512], P(('ctx', 'dp'))
- grad_gain: float32 [4096], P(('ctx', 'dp'))
All inputs are finite; a program needn't handle non-finite values.
Results may differ from a plain program's by a relative error of at most 0.025.
The roundings to bfloat16 on the way count: a program that leaves them out, or rounds other values in their place, can miss the bound.
Values may be sent and summed in bfloat16 or wider, within the bound.
A program may use at most 192 MiB of HBM per device.

v0:
```python
import jax
import jax.numpy as jnp
from jax import lax
from jax.sharding import PartitionSpec as P

KV_HEADS = 4
HEAD_DIM = 128
ROPE_BASE = 500000.0
EPSILON = 1e-05


def positions(span_order, span_len):
    offsets = jnp.arange(span_len, dtype=jnp.int32)
    return (span_order[:, None] * span_len + offsets[None, :]).reshape(-1)


def rotation(token_pos, head_size):
    half_dim = head_size // 2
    frequency = ROPE_BASE ** (-2.0 * jnp.arange(half_dim, dtype=jnp.float32) / head_size)
    angles = token_pos.astype(jnp.float32)[:, None] * frequency[None, :]
    angles = jnp.concatenate([angles, angles], axis=1)
    return (jnp.cos(angles), jnp.sin(angles))


def rotate_half(values):
    half_dim = values.shape[-1] // 2
    return jnp.concatenate([-values[..., half_dim:], values[..., :half_dim]], axis=-1)


def rotate_back(values):
    half_dim = values.shape[-1] // 2
    return jnp.concatenate([values[..., half_dim:], -values[..., :half_dim]], axis=-1)


def normalize(tokens, norm_gain):
    widened = tokens.astype(jnp.float32)
    rms_scale = lax.rsqrt(jnp.mean(widened * widened, axis=-1, keepdims=True) + EPSILON)
    return ((widened * rms_scale * norm_gain).astype(jnp.bfloat16), rms_scale)


def project_keys(normed, key_weight, value_weight, cosine, sine_table, kv_heads, head_size):
    row_count = normed.shape[0]
    key_pre = jnp.dot(normed, key_weight, preferred_element_type=jnp.float32).reshape(
        row_count, kv_heads, head_size
    )
    rotated = key_pre * cosine[:, None, :] + rotate_half(key_pre) * sine_table[:, None, :]
    value_rows = jnp.dot(normed, value_weight, preferred_element_type=jnp.float32)
    return (
        rotated.reshape(row_count, kv_heads * head_size).astype(jnp.bfloat16),
        value_rows.astype(jnp.bfloat16),
    )


def attend_group(query_group, grad_group, key_group, value_group, causal_mask, score_scale):
    scores = (
        jnp.einsum("tgd,sd->gts", query_group, key_group, preferred_element_type=jnp.float32)
        * score_scale
    )
    scores = jnp.where(causal_mask[None], scores, -1e30)
    row_max = jnp.max(scores, axis=-1, keepdims=True)
    exponent = jnp.exp(scores - row_max)
    probability = exponent / jnp.sum(exponent, axis=-1, keepdims=True)
    probability_b = probability.astype(jnp.bfloat16)
    attended = jnp.einsum(
        "gts,sd->tgd", probability_b, value_group, preferred_element_type=jnp.float32
    ).astype(jnp.bfloat16)
    dprob = jnp.einsum("tgd,sd->gts", grad_group, value_group, preferred_element_type=jnp.float32)
    delta = jnp.sum(grad_group.astype(jnp.float32) * attended.astype(jnp.float32), axis=-1)
    dscores = (probability * (dprob - jnp.transpose(delta)[:, :, None])).astype(jnp.bfloat16)
    dquery = (
        jnp.einsum("gts,sd->tgd", dscores, key_group, preferred_element_type=jnp.float32)
        * score_scale
    ).astype(jnp.bfloat16)
    key_term = (
        jnp.einsum("gts,tgd->sd", dscores, query_group, preferred_element_type=jnp.float32)
        * score_scale
    )
    value_term = jnp.einsum(
        "gts,tgd->sd", probability_b, grad_group, preferred_element_type=jnp.float32
    )
    return (attended, dquery, key_term, value_term)


def attend_device(queries, grads, all_keys, all_values, query_pos, key_pos, kv_heads, head_size):
    row_count = queries.shape[0]
    group_size = queries.shape[1] // (kv_heads * head_size)
    group_width = group_size * head_size
    causal_mask = key_pos[None, :] <= query_pos[:, None]
    score_scale = head_size ** (-0.5)
    outputs = []
    for head_group in range(kv_heads):
        query_group = queries[:, head_group * group_width : (head_group + 1) * group_width].reshape(
            row_count, group_size, head_size
        )
        grad_group = grads[:, head_group * group_width : (head_group + 1) * group_width].reshape(
            row_count, group_size, head_size
        )
        key_group = all_keys[:, head_group * head_size : (head_group + 1) * head_size]
        value_group = all_values[:, head_group * head_size : (head_group + 1) * head_size]
        outputs.append(
            attend_group(query_group, grad_group, key_group, value_group, causal_mask, score_scale)
        )
    attended = jnp.concatenate(
        [item[0].reshape(row_count, group_width) for item in outputs], axis=1
    )
    dquery = jnp.concatenate([item[1].reshape(row_count, group_width) for item in outputs], axis=1)
    key_terms = jnp.concatenate([item[2] for item in outputs], axis=1)
    value_terms = jnp.concatenate([item[3] for item in outputs], axis=1)
    return (attended, dquery, key_terms, value_terms)


def finish_backward(
    tokens,
    normed,
    rms_scale,
    key_grad,
    value_grad,
    cosine,
    sine_table,
    norm_gain,
    key_weight,
    value_weight,
    kv_heads,
    head_size,
):
    row_count = tokens.shape[0]
    shaped = key_grad.reshape(row_count, kv_heads, head_size)
    key_pre_grad = (
        (shaped * cosine[:, None, :] + rotate_back(shaped * sine_table[:, None, :]))
        .reshape(row_count, kv_heads * head_size)
        .astype(jnp.bfloat16)
    )
    value_pre_grad = value_grad.astype(jnp.bfloat16)
    weight_key = jnp.dot(normed.T, key_pre_grad, preferred_element_type=jnp.float32)
    weight_value = jnp.dot(normed.T, value_pre_grad, preferred_element_type=jnp.float32)
    normed_grad = jnp.dot(key_pre_grad, key_weight.T, preferred_element_type=jnp.float32) + jnp.dot(
        value_pre_grad, value_weight.T, preferred_element_type=jnp.float32
    )
    widened = tokens.astype(jnp.float32)
    gain_part = jnp.sum(normed_grad * widened * rms_scale, axis=0)
    inner_mean = jnp.mean(normed_grad * norm_gain * widened, axis=-1, keepdims=True)
    grad_rows = (
        rms_scale * norm_gain * normed_grad - widened * rms_scale**3 * inner_mean
    ).astype(jnp.bfloat16)
    return (grad_rows, weight_key, weight_value, gain_part)


def body(tokens, queries, d_attended, span_order, norm_gain, key_weight, value_weight):
    local_seqs = tokens.shape[0]
    row_count = tokens.shape[1]
    model_width = tokens.shape[2]
    kv_width = key_weight.shape[1]
    shard_index = lax.axis_index("ctx")
    token_pos = positions(span_order, row_count // 2)
    query_pos = lax.dynamic_slice_in_dim(token_pos, shard_index * row_count, row_count, 0)
    cosine, sine_table = rotation(query_pos, HEAD_DIM)
    cosine_all = jnp.tile(cosine, (local_seqs, 1))
    sine_all = jnp.tile(sine_table, (local_seqs, 1))
    flat_tokens = tokens.reshape(local_seqs * row_count, model_width)
    normed, rms_scale = normalize(flat_tokens, norm_gain)
    rotated_keys, value_rows = project_keys(
        normed, key_weight, value_weight, cosine_all, sine_all, KV_HEADS, HEAD_DIM
    )
    rotated_keys = rotated_keys.reshape(local_seqs, row_count, kv_width)
    value_rows = value_rows.reshape(local_seqs, row_count, kv_width)
    all_keys, all_values = (
        lax.all_gather(rotated_keys, "ctx", axis=1, tiled=True),
        lax.all_gather(value_rows, "ctx", axis=1, tiled=True),
    )
    attended_list, dquery_list, key_list, value_list = ([], [], [], [])
    for sequence in range(local_seqs):
        attended, dquery, key_terms, value_terms = attend_device(
            queries[sequence],
            d_attended[sequence],
            all_keys[sequence],
            all_values[sequence],
            query_pos,
            token_pos,
            KV_HEADS,
            HEAD_DIM,
        )
        attended_list.append(attended)
        dquery_list.append(dquery)
        key_list.append(key_terms)
        value_list.append(value_terms)
    key_stack = jnp.stack(key_list)
    value_stack = jnp.stack(value_list)
    key_grad, value_grad = (
        lax.psum_scatter(
            key_stack.astype(jnp.bfloat16), "ctx", scatter_dimension=1, tiled=True
        ).astype(jnp.float32),
        lax.psum_scatter(
            value_stack.astype(jnp.bfloat16), "ctx", scatter_dimension=1, tiled=True
        ).astype(jnp.float32),
    )
    key_grad = key_grad.reshape(local_seqs * row_count, kv_width)
    value_grad = value_grad.reshape(local_seqs * row_count, kv_width)
    grad_rows, weight_key, weight_value, gain_part = finish_backward(
        flat_tokens,
        normed,
        rms_scale,
        key_grad,
        value_grad,
        cosine_all,
        sine_all,
        norm_gain,
        key_weight,
        value_weight,
        KV_HEADS,
        HEAD_DIM,
    )
    weight_key, weight_value, gain_part = (
        lax.psum_scatter(
            weight_key.astype(jnp.bfloat16), "ctx", scatter_dimension=0, tiled=True
        ).astype(jnp.float32),
        lax.psum_scatter(
            weight_value.astype(jnp.bfloat16), "ctx", scatter_dimension=0, tiled=True
        ).astype(jnp.float32),
        lax.psum_scatter(
            gain_part.astype(jnp.bfloat16), "ctx", scatter_dimension=0, tiled=True
        ).astype(jnp.float32),
    )
    weight_key, weight_value, gain_part = (
        lax.psum_scatter(
            weight_key.astype(jnp.bfloat16), "dp", scatter_dimension=0, tiled=True
        ).astype(jnp.float32),
        lax.psum_scatter(
            weight_value.astype(jnp.bfloat16), "dp", scatter_dimension=0, tiled=True
        ).astype(jnp.float32),
        lax.psum_scatter(
            gain_part.astype(jnp.bfloat16), "dp", scatter_dimension=0, tiled=True
        ).astype(jnp.float32),
    )
    return (
        jnp.stack(attended_list),
        jnp.stack(dquery_list),
        grad_rows.reshape(local_seqs, row_count, model_width),
        weight_key,
        weight_value,
        gain_part,
    )


def solution(mesh):
    placed = (P("dp", "ctx", None), P("dp", "ctx", None), P("dp", "ctx", None), P(), P(), P(), P())
    return jax.shard_map(
        body,
        mesh=mesh,
        in_specs=placed,
        out_specs=(
            P("dp", "ctx", None),
            P("dp", "ctx", None),
            P("dp", "ctx", None),
            P(("ctx", "dp"), None),
            P(("ctx", "dp"), None),
            P(("ctx", "dp")),
        ),
        check_vma=False,
    )
```

profile of v0, /device:TPU:0, one launch (start us, length us, event | category | flops | bytes accessed | tf_op | source)
XLA Modules:
  0.0 512.8 jit_solution(5786807104449921285)
XLA Ops:
  10.2 6.5 %copy.154 = bf16[512,4096]{1,0:T(8,128)(2,1)} copy(bf16[512,4096]{0,1:T(8,128)(2,1)} %bitcast.753) | data formatting | bytes 8388608 | tf_op jit(solution)/shard_map/dot_general | solution.py:43
  17.0 3.4 fusion.276
  21.9 3.7 convolution_convert_fusion.1
  27.7 36.9 %all-gather.5.cloned.1.call-done = bf16[2,512,512]{2,1,0:T(8,128)(2,1)} async-done(((bf16[2,64,512]{2,1,0:T(8,128)(2,1)}), bf16[2,512,512]{2,1,0:T(8,128)(2,1)}) %all-gather.5.cloned.1.call-update) | async-done | bytes 1048592 | tf_op jit(solution)/shard_map/all_gather | solution.py:167
  70.5 35.8 %all-gather.3.cloned.1.call-done = bf16[2,512,512]{2,1,0:T(8,128)(2,1)} async-done(((bf16[2,64,512]{2,1,0:T(8,128)(2,1)}), bf16[2,512,512]{2,1,0:T(8,128)(2,1)}) %all-gather.3.cloned.1.call-update) | async-done | bytes 1048592 | tf_op jit(solution)/shard_map/all_gather | solution.py:168
  113.6 2.4 multiply_reduce_fusion.5
  120.6 2.4 multiply_reduce_fusion.6
  123.9 2.4 fusion.273
  127.5 2.4 multiply_reduce_fusion.7
  130.8 2.5 fusion.252
  136.8 2.5 fusion.255
  142.8 2.4 fusion.258
  163.6 2.1 copy.150
  168.1 2.1 copy.137
  172.1 99.3 %all-reduce.7.cloned.1.call-done = (bf16[2,512,512]{2,0,1:T(2,128)(2,1)}, bf16[2,512,512]{2,0,1:T(2,128)(2,1)}) async-done(((bf16[2,512,512]{2,0,1:T(2,128)(2,1)}, bf16[2,512,512]{2,0,1:T(2,128)(2,1)}), (bf16[2,512,512]{2,0,1:T(2,128)(2,1)}, bf16[2,512,512]{2,0,1:T(2,128)(2,1)})) %all-reduce.7.cloned.1.call-update) | async-done | bytes 2097168
  273.4 3.2 convolution_convert_fusion
  277.8 3.3 bitcast_convert_fusion
  295.8 68.7 %reduce-scatter.5.cloned.1.call-done = bf16[512,512]{1,0:T(8,128)(2,1)} async-done(((bf16[4096,512]{1,0:T(8,128)(2,1)}), bf16[512,512]{1,0:T(8,128)(2,1)}) %reduce-scatter.5.cloned.1.call-update) | async-done | bytes 524304 | tf_op jit(solution)/shard_map/reduce_scatter | solution.py:213
  364.6 3.8 fusion.277
  370.2 21.3 %all-reduce.2 = bf16[4096]{0:T(1024)(128)(2,1)S(1)} all-reduce(bf16[4096]{0:T(1024)(128)(2,1)S(1)} %get-tuple-element.6), channel_id=8, replica_groups=mesh['ctx'=8,'dp'=4] {'ctx'}, use_global_device_ids=true, to_apply=%region_33.34.clone | all-reduce | flops 4096 | bytes 16384
  391.6 6.0 %all-reduce.3 = bf16[512]{0:T(512)(128)(2,1)S(1)} all-reduce(bf16[512]{0:T(512)(128)(2,1)S(1)} %dynamic-slice.5), channel_id=9, replica_groups=mesh['ctx'=8,'dp'=4] {'dp'}, use_global_device_ids=true, to_apply=%region_34.35.clone | all-reduce | flops 512 | bytes 2048
  397.7 58.8 %reduce-scatter.9.cloned.1.call-done = bf16[512,512]{1,0:T(8,128)(2,1)} async-done(((bf16[4096,512]{1,0:T(8,128)(2,1)}), bf16[512,512]{1,0:T(8,128)(2,1)}) %reduce-scatter.9.cloned.1.call-update) | async-done | bytes 524304 | tf_op jit(solution)/shard_map/reduce_scatter | solution.py:216
  458.7 21.4 %reduce-scatter.7.cloned.1.call-done = bf16[128,512]{1,0:T(8,128)(2,1)} async-done(((bf16[512,512]{1,0:T(8,128)(2,1)}), bf16[128,512]{1,0:T(8,128)(2,1)}) %reduce-scatter.7.cloned.1.call-update) | async-done | bytes 131088 | tf_op jit(solution)/shard_map/reduce_scatter | solution.py:224
  481.7 22.5 %reduce-scatter.11.cloned.1.call-done = bf16[128,512]{1,0:T(8,128)(2,1)} async-done(((bf16[512,512]{1,0:T(8,128)(2,1)}), bf16[128,512]{1,0:T(8,128)(2,1)}) %reduce-scatter.11.cloned.1.call-update) | async-done | bytes 131088 | tf_op jit(solution)/shard_map/reduce_scatter | solution.py:227
  (343 shorter events, 79.2 us)
Async XLA Ops:
  7.2 57.4 %all-gather.5.cloned.1.call-start = ((), (), s32[]{:S(2)}) async-start(), calls=%async_computation.5 | async-start | bytes 1179648 | tf_op jit(solution)/shard_map/all_gather | solution.py:167
  21.4 84.9 %all-gather.3.cloned.1.call-start = ((), (), s32[]{:S(2)}) async-start(), calls=%async_computation.4 | async-start | bytes 1179648 | tf_op jit(solution)/shard_map/all_gather | solution.py:168
  25.6 245.8 %all-reduce.7.cloned.1.call-start = ((), (), s32[]{:S(2)}) async-start(), calls=%async_computation.10 | async-start | bytes 4194304
  26.7 39.2 %copy-start.69 = (bf16[8,4,8,128]{3,2,1,0:T(8,128)(2,1)}, bf16[8,4,8,128]{3,2,1,0:T(8,128)(2,1)S(1)}, u32[]{:S(2)}) copy-start(bf16[8,4,8,128]{3,2,1,0:T(8,128)(2,1)S(1)} %get-tuple-element.83) | copy-start | bytes 196612
  26.8 39.1 %copy-start.79 = (pred[64,512]{1,0:T(8,128)(4,1)}, pred[64,512]{1,0:T(8,128)(4,1)S(1)}, u32[]{:S(2)}) copy-start(pred[64,512]{1,0:T(8,128)(4,1)S(1)} %broadcast_compare_fusion) | copy-start | bytes 98308
  65.8 58.0 %copy-start.4 = (bf16[512,512]{1,0:T(8,128)(2,1)}, bf16[512,512]{1,0:T(8,128)(2,1)S(1)}, u32[]{:S(2)}) copy-start(bf16[512,512]{1,0:T(8,128)(2,1)S(1)} %get-tuple-element.14) | copy-start | bytes 1572868
  65.8 82.9 %copy-start.2 = (bf16[512,512]{1,0:T(8,128)(2,1)}, bf16[512,512]{1,0:T(8,128)(2,1)S(1)}, u32[]{:S(2)}) copy-start(bf16[512,512]{1,0:T(8,128)(2,1)S(1)} %get-tuple-element.15) | copy-start | bytes 1572868
  111.8 8.8 %copy-start.29 = (bf16[8,4,8,128]{3,2,1,0:T(8,128)(2,1)S(1)}, bf16[8,4,8,128]{3,2,1,0:T(8,128)(2,1)}, u32[]{:S(2)}) copy-start(bf16[8,4,8,128]{3,2,1,0:T(8,128)(2,1)} %get-tuple-element.77) | copy-start | bytes 196612
  113.5 10.3 %copy-start.65 = (bf16[8,4,8,128]{3,2,1,0:T(8,128)(2,1)S(1)}, bf16[8,4,8,128]{3,2,1,0:T(8,128)(2,1)}, u32[]{:S(2)}) copy-start(bf16[8,4,8,128]{3,2,1,0:T(8,128)(2,1)} %get-tuple-element.84) | copy-start | bytes 196612
  118.8 8.7 %copy-start.27 = (bf16[8,4,8,128]{3,2,1,0:T(8,128)(2,1)S(1)}, bf16[8,4,8,128]{3,2,1,0:T(8,128)(2,1)}, u32[]{:S(2)}) copy-start(bf16[8,4,8,128]{3,2,1,0:T(8,128)(2,1)} %get-tuple-element.80) | copy-start | bytes 196612
  120.5 10.2 %copy-start.63 = (bf16[8,4,8,128]{3,2,1,0:T(8,128)(2,1)S(1)}, bf16[8,4,8,128]{3,2,1,0:T(8,128)(2,1)}, u32[]{:S(2)}) copy-start(bf16[8,4,8,128]{3,2,1,0:T(8,128)(2,1)} %get-tuple-element.37) | copy-start | bytes 196612
  126.3 8.1 %copy-start.25 = (bf16[8,4,8,128]{3,2,1,0:T(8,128)(2,1)S(1)}, bf16[8,4,8,128]{3,2,1,0:T(8,128)(2,1)}, u32[]{:S(2)}) copy-start(bf16[8,4,8,128]{3,2,1,0:T(8,128)(2,1)} %get-tuple-element.29) | copy-start | bytes 196612
  126.3 9.1 %copy-start.6 = (bf16[512,512]{1,0:T(8,128)(2,1)S(1)}, bf16[512,512]{1,0:T(8,128)(2,1)}, u32[]{:S(2)}) copy-start(bf16[512,512]{1,0:T(8,128)(2,1)} %get-tuple-element.13) | copy-start | bytes 1572868
  127.5 9.3 %copy-start.61 = (bf16[8,4,8,128]{3,2,1,0:T(8,128)(2,1)S(1)}, bf16[8,4,8,128]{3,2,1,0:T(8,128)(2,1)}, u32[]{:S(2)}) copy-start(bf16[8,4,8,128]{3,2,1,0:T(8,128)(2,1)} %get-tuple-element.38) | copy-start | bytes 196612
  133.2 7.2 %copy-start.23 = (bf16[8,4,8,128]{3,2,1,0:T(8,128)(2,1)S(1)}, bf16[8,4,8,128]{3,2,1,0:T(8,128)(2,1)}, u32[]{:S(2)}) copy-start(bf16[8,4,8,128]{3,2,1,0:T(8,128)(2,1)} %get-tuple-element.30) | copy-start | bytes 196612
  134.4 8.4 %copy-start.59 = (bf16[8,4,8,128]{3,2,1,0:T(8,128)(2,1)S(1)}, bf16[8,4,8,128]{3,2,1,0:T(8,128)(2,1)}, u32[]{:S(2)}) copy-start(bf16[8,4,8,128]{3,2,1,0:T(8,128)(2,1)} %get-tuple-element.39) | copy-start | bytes 196612
  139.3 7.2 %copy-start.21 = (bf16[8,4,8,128]{3,2,1,0:T(8,128)(2,1)S(1)}, bf16[8,4,8,128]{3,2,1,0:T(8,128)(2,1)}, u32[]{:S(2)}) copy-start(bf16[8,4,8,128]{3,2,1,0:T(8,128)(2,1)} %get-tuple-element.31) | copy-start | bytes 196612
  140.4 8.3 %copy-start.57 = (bf16[8,4,8,128]{3,2,1,0:T(8,128)(2,1)S(1)}, bf16[8,4,8,128]{3,2,1,0:T(8,128)(2,1)}, u32[]{:S(2)}) copy-start(bf16[8,4,8,128]{3,2,1,0:T(8,128)(2,1)} %get-tuple-element.36) | copy-start | bytes 196612
  170.2 194.3 %reduce-scatter.5.cloned.1.call-start = ((), (), s32[]{:S(2)}) async-start(), calls=%async_computation.6 | async-start | bytes 4718592 | tf_op jit(solution)/shard_map/reduce_scatter | solution.py:213
  276.7 179.8 %reduce-scatter.9.cloned.1.call-start = ((), (), s32[]{:S(2)}) async-start(), calls=%async_computation.8 | async-start | bytes 4718592 | tf_op jit(solution)/shard_map/reduce_scatter | solution.py:216
  281.1 7.6 %copy-start.3 = (bf16[512,512]{1,0:T(8,128)(2,1)S(1)}, bf16[512,512]{1,0:T(8,128)(2,1)}, u32[]{:S(2)}) copy-start(bf16[512,512]{1,0:T(8,128)(2,1)} %copy-done.2) | copy-start | bytes 1572868
  281.1 199.0 %reduce-scatter.7.cloned.1.call-start = ((), (), s32[]{:S(2)}) async-start(), calls=%async_computation.7 | async-start | bytes 655360 | tf_op jit(solution)/shard_map/reduce_scatter | solution.py:224
  364.6 139.7 %reduce-scatter.11.cloned.1.call-start = ((), (), s32[]{:S(2)}) async-start(), calls=%async_computation.9 | async-start | bytes 655360 | tf_op jit(solution)/shard_map/reduce_scatter | solution.py:227
  368.5 88.6 %copy-start.98 = (f32[128]{0:T(128)S(1)}, f32[128]{0:T(128)}, u32[]{:S(2)}) copy-start(f32[128]{0:T(128)} %multiply_multiply_fusion) | copy-start | bytes 1540
  (84 other events, 258.2 us)
Sparse Core Ops, SparseCore 0:
  21.6 42.9 all-gather.4
  67.3 38.9 all-gather.2
  170.3 101.0 all-reduce.6
  276.8 87.6 reduce-scatter.4
  368.0 88.4 reduce-scatter.8
  458.8 21.2 reduce-scatter.6
  482.6 21.6 reduce-scatter.10
where the time goes:
time: 514 us; the launch traced here: 513 us
  waiting for transfers between devices  344 us (67%)
  matrix products  75.4 us (15%)
  blocking collectives  27.4 us (5%)
  local copies, waits for them, and re-layouts  26.2 us (5%)
  other arithmetic  21.8 us (4%)
  between operations  17.6 us (3%)
    unnamed x8, waiting for transfers between devices  99.4 us
    reduce_scatter x1, waiting for transfers between devices, body(): lax.psum_scatter(weight_key.astype(jnp.bfloat16), 'ctx', scatter_dimensio...  68.7 us
    reduce_scatter x1, waiting for transfers between devices, body(): lax.psum_scatter(weight_value.astype(jnp.bfloat16), 'ctx', scatter_dimens...  58.8 us
    all_gather x1, waiting for transfers between devices, body(): lax.all_gather(rotated_keys, 'ctx', axis=1, tiled=True)  36.9 us
    all_gather x1, waiting for transfers between devices, body(): lax.all_gather(value_rows, 'ctx', axis=1, tiled=True)  35.8 us
    unnamed x2, blocking collectives  27.4 us
    reduce_scatter x1, waiting for transfers between devices, body(): lax.psum_scatter(weight_value.astype(jnp.bfloat16), 'dp', scatter_dimensi...  22.5 us
    reduce_scatter x1, waiting for transfers between devices, body(): lax.psum_scatter(weight_key.astype(jnp.bfloat16), 'dp', scatter_dimension...  21.4 us
  transfers between devices with their start and end apart: 7, of which 7 were waited for; matrix products, arithmetic and copies ran while one was open for 8% of the time, Pallas kernels for 0%

commit v1 on v0

--- a/solution.py
+++ b/solution.py
@@ -7,6 +7,7 @@
 HEAD_DIM = 128
 ROPE_BASE = 500000.0
 EPSILON = 1e-05
+end_floor = lambda where_dim, own_rows: jnp.concatenate(lax.all_gather(own_rows, "ctx"), where_dim)
 
 
 def positions(span_order, span_len):
@@ -165,7 +166,7 @@
     value_rows = value_rows.reshape(local_seqs, row_count, kv_width)
     all_keys, all_values = (
         lax.all_gather(rotated_keys, "ctx", axis=1, tiled=True),
-        lax.all_gather(value_rows, "ctx", axis=1, tiled=True),
+        end_floor(1, value_rows),
     )
     attended_list, dquery_list, key_list, value_list = ([], [], [], [])
     for sequence in range(local_seqs):

time: 514 us -> 516 us (level)
  waiting for transfers between devices: 344 us -> 334 us
  matrix products: 75.4 us -> 81.1 us
    all_gather x1, waiting for transfers between devices: 35.8 us -> 27.2 us  [lax.all_gather(own_rows, 'ctx')]
  transfers between devices with their start and end apart: 7 -> 7, of which waited for: 7 -> 7; matrix products, arithmetic and copies ran while one was open for 8% -> 9% of each run, Pallas kernels for 0% -> 0%
where the time goes in v1:
time: 516 us; the launch traced here: 514 us
  waiting for transfers between devices  334 us (65%)
  matrix products  81.1 us (16%)
  blocking collectives  27.7 us (5%)
  local copies, waits for them, and re-layouts  26.6 us (5%)
  other arithmetic  25.7 us (5%)
  between operations  17.6 us (3%)
    unnamed x8, waiting for transfers between devices  99.5 us
    reduce_scatter x1, waiting for transfers between devices, body(): lax.psum_scatter(weight_key.astype(jnp.bfloat16), 'ctx', scatter_dimensio...  68.6 us
    reduce_scatter x1, waiting for transfers between devices, body(): lax.psum_scatter(weight_value.astype(jnp.bfloat16), 'ctx', scatter_dimens...  57.3 us
    all_gather x1, waiting for transfers between devices, body(): lax.all_gather(rotated_keys, 'ctx', axis=1, tiled=True)  39.5 us
    unnamed x2, blocking collectives  27.7 us
    all_gather x1, waiting for transfers between devices, lax.all_gather(own_rows, 'ctx')  27.2 us
    reduce_scatter x1, waiting for transfers between devices, body(): lax.psum_scatter(weight_value.astype(jnp.bfloat16), 'dp', scatter_dimensi...  22.5 us
    reduce_scatter x1, waiting for transfers between devices, body(): lax.psum_scatter(weight_key.astype(jnp.bfloat16), 'dp', scatter_dimension...  19.9 us
  transfers between devices with their start and end apart: 7, of which 7 were waited for; matrix products, arithmetic and copies ran while one was open for 9% of the time, Pallas kernels for 0%

profile of v1, /device:TPU:0, one launch (start us, length us, event | category | flops | bytes accessed | tf_op | source)
XLA Modules:
  0.0 513.9 jit_solution(16306066705791413198)
XLA Ops:
  10.4 3.6 convolution_convert_fusion.1
  15.4 6.5 %copy.154 = bf16[512,4096]{1,0:T(8,128)(2,1)} copy(bf16[512,4096]{0,1:T(8,128)(2,1)} %bitcast.752) | data formatting | bytes 8388608 | tf_op jit(solution)/shard_map/dot_general | solution.py:44
  22.2 3.5 fusion.277
  30.0 27.2 %all-gather.3.cloned.1.call-done = bf16[8,2,64,512]{3,2,1,0:T(8,128)(2,1)} async-done(((bf16[1,2,64,512]{3,2,1,0:T(8,128)(2,1)}), bf16[8,2,64,512]{3,2,1,0:T(8,128)(2,1)}) %all-gather.3.cloned.1.call-update) | async-done | bytes 1048592 | tf_op jit(solution)/shard_map/all_gather | solution.py:10
  59.4 39.5 %all-gather.5.cloned.1.call-done = bf16[2,512,512]{2,1,0:T(8,128)(2,1)} async-done(((bf16[2,64,512]{2,1,0:T(8,128)(2,1)}), bf16[2,512,512]{2,1,0:T(8,128)(2,1)}) %all-gather.5.cloned.1.call-update) | async-done | bytes 1048592 | tf_op jit(solution)/shard_map/all_gather | solution.py:168
  100.2 2.6 fusion.265
  105.7 2.4 multiply_reduce_fusion.4
  108.1 2.5 fusion.268
  115.8 2.5 fusion.271
  123.5 2.5 fusion.274
  127.2 2.3 multiply_reduce_fusion.7
  131.3 2.5 fusion.253
  173.1 99.4 %all-reduce.7.cloned.1.call-done = (bf16[2,512,512]{2,0,1:T(2,128)(2,1)}, bf16[2,512,512]{2,0,1:T(2,128)(2,1)}) async-done(((bf16[2,512,512]{2,0,1:T(2,128)(2,1)}, bf16[2,512,512]{2,0,1:T(2,128)(2,1)}), (bf16[2,512,512]{2,0,1:T(2,128)(2,1)}, bf16[2,512,512]{2,0,1:T(2,128)(2,1)})) %all-reduce.7.cloned.1.call-update) | async-done | bytes 2097168
  274.5 3.3 convolution_convert_fusion
  278.9 3.3 bitcast_convert_fusion
  297.0 68.6 %reduce-scatter.5.cloned.1.call-done = bf16[512,512]{1,0:T(8,128)(2,1)} async-done(((bf16[4096,512]{1,0:T(8,128)(2,1)}), bf16[512,512]{1,0:T(8,128)(2,1)}) %reduce-scatter.5.cloned.1.call-update) | async-done | bytes 524304 | tf_op jit(solution)/shard_map/reduce_scatter | solution.py:214
  365.7 3.8 fusion.278
  369.5 3.0 fusion.18
  372.5 21.7 %all-reduce.2 = bf16[4096]{0:T(1024)(128)(2,1)S(1)} all-reduce(bf16[4096]{0:T(1024)(128)(2,1)S(1)} %get-tuple-element.6), channel_id=8, replica_groups=mesh['ctx'=8,'dp'=4] {'ctx'}, use_global_device_ids=true, to_apply=%region_33.34.clone | all-reduce | flops 4096 | bytes 16384
  394.3 6.0 %all-reduce.3 = bf16[512]{0:T(512)(128)(2,1)S(1)} all-reduce(bf16[512]{0:T(512)(128)(2,1)S(1)} %dynamic-slice.5), channel_id=9, replica_groups=mesh['ctx'=8,'dp'=4] {'dp'}, use_global_device_ids=true, to_apply=%region_34.35.clone | all-reduce | flops 512 | bytes 2048
  400.4 57.3 %reduce-scatter.9.cloned.1.call-done = bf16[512,512]{1,0:T(8,128)(2,1)} async-done(((bf16[4096,512]{1,0:T(8,128)(2,1)}), bf16[512,512]{1,0:T(8,128)(2,1)}) %reduce-scatter.9.cloned.1.call-update) | async-done | bytes 524304 | tf_op jit(solution)/shard_map/reduce_scatter | solution.py:217
  458.2 3.2 fusion.15
  461.4 19.9 %reduce-scatter.7.cloned.1.call-done = bf16[128,512]{1,0:T(8,128)(2,1)} async-done(((bf16[512,512]{1,0:T(8,128)(2,1)}), bf16[128,512]{1,0:T(8,128)(2,1)}) %reduce-scatter.7.cloned.1.call-update) | async-done | bytes 131088 | tf_op jit(solution)/shard_map/reduce_scatter | solution.py:225
  482.9 22.5 %reduce-scatter.11.cloned.1.call-done = bf16[128,512]{1,0:T(8,128)(2,1)} async-done(((bf16[512,512]{1,0:T(8,128)(2,1)}), bf16[128,512]{1,0:T(8,128)(2,1)}) %reduce-scatter.11.cloned.1.call-update) | async-done | bytes 131088 | tf_op jit(solution)/shard_map/reduce_scatter | solution.py:228
  (325 shorter events, 86.7 us)
Async XLA Ops:
  7.2 50.0 %all-gather.3.cloned.1.call-start = ((), (), s32[]{:S(2)}) async-start(), calls=%async_computation.4 | async-start | bytes 1179648 | tf_op jit(solution)/shard_map/all_gather | solution.py:10
  14.0 84.9 %all-gather.5.cloned.1.call-start = ((), (), s32[]{:S(2)}) async-start(), calls=%async_computation.5 | async-start | bytes 1179648 | tf_op jit(solution)/shard_map/all_gather | solution.py:168
  15.3 6.5 %copy-start = (bf16[2,64,4096]{2,1,0:T(8,128)(2,1)S(1)}, bf16[2,64,4096]{2,1,0:T(8,128)(2,1)}, u32[]{:S(2)}) copy-start(bf16[2,64,4096]{2,1,0:T(8,128)(2,1)} %param.7) | copy-start | bytes 3145732
  15.4 6.5 %copy-start.51 = (f32[4096]{0:T(1024)S(1)}, f32[4096]{0:T(1024)}, u32[]{:S(2)}) copy-start(f32[4096]{0:T(1024)} %param.11) | copy-start | bytes 49156
  26.7 245.8 %all-reduce.7.cloned.1.call-start = ((), (), s32[]{:S(2)}) async-start(), calls=%async_computation.10 | async-start | bytes 4194304
  29.9 105.9 %copy-start.24 = (bf16[8,4,8,128]{3,2,1,0:T(8,128)(2,1)}, bf16[8,4,8,128]{3,2,1,0:T(8,128)(2,1)S(1)}, u32[]{:S(2)}) copy-start(bf16[8,4,8,128]{3,2,1,0:T(8,128)(2,1)S(1)} %get-tuple-element.29) | copy-start | bytes 196612
  29.9 112.6 %copy-start.22 = (bf16[8,4,8,128]{3,2,1,0:T(8,128)(2,1)}, bf16[8,4,8,128]{3,2,1,0:T(8,128)(2,1)S(1)}, u32[]{:S(2)}) copy-start(bf16[8,4,8,128]{3,2,1,0:T(8,128)(2,1)S(1)} %get-tuple-element.30) | copy-start | bytes 196612
  29.9 118.0 %copy-start.20 = (bf16[8,4,8,128]{3,2,1,0:T(8,128)(2,1)}, bf16[8,4,8,128]{3,2,1,0:T(8,128)(2,1)S(1)}, u32[]{:S(2)}) copy-start(bf16[8,4,8,128]{3,2,1,0:T(8,128)(2,1)S(1)} %get-tuple-element.31) | copy-start | bytes 196612
  29.9 123.5 %copy-start.19 = (bf16[8,4,8,128]{3,2,1,0:T(8,128)(2,1)}, bf16[8,4,8,128]{3,2,1,0:T(8,128)(2,1)S(1)}, u32[]{:S(2)}) copy-start(bf16[8,4,8,128]{3,2,1,0:T(8,128)(2,1)S(1)} %get-tuple-element.28) | copy-start | bytes 196612
  100.2 23.3 %copy-start.4 = (bf16[512,512]{1,0:T(8,128)(2,1)}, bf16[512,512]{1,0:T(8,128)(2,1)S(1)}, u32[]{:S(2)}) copy-start(bf16[512,512]{1,0:T(8,128)(2,1)S(1)} %get-tuple-element.14) | copy-start | bytes 1572868
  100.2 48.6 %copy-start.2 = (bf16[512,512]{1,0:T(8,128)(2,1)}, bf16[512,512]{1,0:T(8,128)(2,1)S(1)}, u32[]{:S(2)}) copy-start(bf16[512,512]{1,0:T(8,128)(2,1)S(1)} %get-tuple-element.15) | copy-start | bytes 1572868
  126.0 9.9 %copy-start.6 = (bf16[1,8,64,512]{3,2,0,1:T(8,128)(2,1)S(1)}, bf16[1,8,64,512]{3,2,0,1:T(8,128)(2,1)}, u32[]{:S(2)}) copy-start(bf16[1,8,64,512]{3,2,0,1:T(8,128)(2,1)} %get-tuple-element.13) | copy-start | bytes 1572868
  141.0 7.8 %copy-start.52 = (bf16[8,4,8,128]{3,2,1,0:T(8,128)(2,1)S(1)}, bf16[8,4,8,128]{3,2,1,0:T(8,128)(2,1)}, u32[]{:S(2)}) copy-start(bf16[8,4,8,128]{3,2,1,0:T(8,128)(2,1)} %get-tuple-element.36) | copy-start | bytes 196612
  145.4 8.1 %copy-start.85 = (f32[4,64]{1,0:T(4,128)}, f32[4,64]{1,0:T(4,128)S(1)}, u32[]{:S(2)}) copy-start(f32[4,64]{1,0:T(4,128)S(1)} %get-tuple-element.48) | copy-start | bytes 3076
  171.2 194.4 %reduce-scatter.5.cloned.1.call-start = ((), (), s32[]{:S(2)}) async-start(), calls=%async_computation.6 | async-start | bytes 4718592 | tf_op jit(solution)/shard_map/reduce_scatter | solution.py:214
  277.9 179.8 %reduce-scatter.9.cloned.1.call-start = ((), (), s32[]{:S(2)}) async-start(), calls=%async_computation.8 | async-start | bytes 4718592 | tf_op jit(solution)/shard_map/reduce_scatter | solution.py:217
  282.2 7.7 %copy-start.3 = (bf16[512,512]{1,0:T(8,128)(2,1)S(1)}, bf16[512,512]{1,0:T(8,128)(2,1)}, u32[]{:S(2)}) copy-start(bf16[512,512]{1,0:T(8,128)(2,1)} %copy-done.2) | copy-start | bytes 1572868
  282.2 199.1 %reduce-scatter.7.cloned.1.call-start = ((), (), s32[]{:S(2)}) async-start(), calls=%async_computation.7 | async-start | bytes 655360 | tf_op jit(solution)/shard_map/reduce_scatter | solution.py:225
  288.1 6.7 %copy-start.61 = (bf16[128,4,64]{0,2,1:T(8,128)(2,1)S(1)}, bf16[128,4,64]{0,2,1:T(8,128)(2,1)}, u32[]{:S(2)}) copy-start(bf16[128,4,64]{0,2,1:T(8,128)(2,1)} %get-tuple-element.69) | copy-start | bytes 196612
  288.1 6.7 %copy-start.62 = (bf16[128,4,64]{0,2,1:T(8,128)(2,1)S(1)}, bf16[128,4,64]{0,2,1:T(8,128)(2,1)}, u32[]{:S(2)}) copy-start(bf16[128,4,64]{0,2,1:T(8,128)(2,1)} %get-tuple-element.71) | copy-start | bytes 196612
  288.1 6.7 %copy-start.63 = (bf16[128,4,64]{0,2,1:T(8,128)(2,1)S(1)}, bf16[128,4,64]{0,2,1:T(8,128)(2,1)}, u32[]{:S(2)}) copy-start(bf16[128,4,64]{0,2,1:T(8,128)(2,1)} %get-tuple-element.73) | copy-start | bytes 196612
  288.4 6.5 %copy-start.67 = (bf16[128,4,64]{0,2,1:T(8,128)(2,1)S(1)}, bf16[128,4,64]{0,2,1:T(8,128)(2,1)}, u32[]{:S(2)}) copy-start(bf16[128,4,64]{0,2,1:T(8,128)(2,1)} %get-tuple-element.65) | copy-start | bytes 196612
  365.6 139.8 %reduce-scatter.11.cloned.1.call-start = ((), (), s32[]{:S(2)}) async-start(), calls=%async_computation.9 | async-start | bytes 655360 | tf_op jit(solution)/shard_map/reduce_scatter | solution.py:228
  369.5 88.7 %copy-start.88 = (f32[128]{0:T(128)S(1)}, f32[128]{0:T(128)}, u32[]{:S(2)}) copy-start(f32[128]{0:T(128)} %multiply_multiply_fusion) | copy-start | bytes 1540
  (75 other events, 216.6 us)
Sparse Core Ops, SparseCore 0:
  14.1 42.9 all-gather.2
  59.9 38.9 all-gather.4
  171.3 101.0 all-reduce.6
  278.0 87.5 reduce-scatter.4
  369.1 88.5 reduce-scatter.8
  460.0 21.2 reduce-scatter.6
  483.8 21.6 reduce-scatter.10
